TPU v7x, 32 devices: a whole 2x2x4 slice. The times are simulated.
32 devices in a mesh: grp: 2 (over y), tok: 4 (over z), feat: 4 (over x, core).
Axes of the slice: x: 2, y: 2, z: 4, core: 2. Of those that a mesh axis runs over, the one named last changes fastest.
Arguments:
- acts: bfloat16 [6144, 28672], P(('grp', 'tok'), 'feat'), parts along dimension 0, may hold values from -6 to 6
- grads: bfloat16 [6144, 8192], P(('grp', 'tok'), 'feat'), parts along dimension 0, may hold values from -6 to 6
- proj_in: bfloat16 [28672, 512], P('feat'), may hold values from -0.03125 to 0.03125
- proj_out: bfloat16 [8192, 512], P('feat'), may hold values from -0.0625 to 0.0625
- doc_lengths: int32 [8], P('grp'), parts along dimension 0, may hold values from 1 to 1536, 3072 in all
- doc_owner: int32 [8], P('grp'), parts along dimension 0, may hold values from 0 to 3, as said below
Outputs:
- doc_grads: float32 [8, 512, 512], P(('grp', 'tok'), 'feat'), parts along dimension 0
There are 2 independent parts, one for each index of `grp`. A program takes and returns all parts, laid end to end along the dimension named above; an argument that names none is the same for every part. Nothing has to cross between parts.
Inputs may be any that keep to these rules, and one draw needn't show every extreme that they name: `doc_lengths`: the lengths sum to 3072; the largest is exactly 1536. `doc_owner`: every index along tok owns exactly 1 documents.
All inputs are finite; a program needn't handle non-finite values.
Results may differ from a plain program's by a relative error of at most 0.0043.
Values may be sent and summed in bfloat16 or wider, within the bound.
No kernel may reach another device: no remote copies, remote signals or barrier semaphores. Data moves between devices by JAX's collectives and lax.ppermute only.
A program may use at most 64 MiB of HBM per device.

v0:
```python
import jax
import jax.numpy as jnp
from jax import lax
from jax.sharding import PartitionSpec as P


def outer_sum(weight_cols, low_out, low_in):
    width = weight_cols.shape[1]
    row_share = low_out.shape[1]
    weighted = (low_out[:, None, :] * weight_cols[:, :, None]).reshape(
        low_out.shape[0], width * row_share
    )
    product = lax.dot_general(
        weighted, low_in, (((0,), (0,)), ((), ())), preferred_element_type=jnp.float32
    )
    return product.reshape(width, row_share, low_in.shape[1])


def shards(acts, grads, proj_in, proj_out, doc_lengths, doc_owner):
    tok_rows = acts.shape[0]
    doc_count = doc_lengths.shape[0]
    slot_count = doc_count // lax.axis_size("tok")
    part_in = jnp.dot(acts, proj_in, preferred_element_type=jnp.float32)
    part_out = jnp.dot(grads, proj_out, preferred_element_type=jnp.float32)
    full_in = lax.psum(part_in, "feat")
    grad_part = lax.psum_scatter(part_out, "feat", scatter_dimension=1, tiled=True)
    in_low = full_in.astype(jnp.bfloat16)
    out_low = grad_part.astype(jnp.bfloat16)
    doc_ends = jnp.cumsum(doc_lengths)
    doc_starts = doc_ends - doc_lengths
    doc_index = jnp.arange(doc_count, dtype=jnp.int32)
    same_owner = doc_owner[:, None] == doc_owner[None, :]
    earlier = doc_index[:, None] < doc_index[None, :]
    slot_rank = jnp.sum((same_owner & earlier).astype(jnp.int32), axis=0)
    target = doc_owner * slot_count + slot_rank
    matches = target[:, None] == doc_index[None, :]
    routing = matches.astype(jnp.bfloat16)
    own_first = lax.axis_index("tok") * slot_count
    position = lax.axis_index("tok") * tok_rows + jnp.arange(tok_rows, dtype=jnp.int32)
    member = (
        (position[:, None] >= doc_starts[None, :]) & (position[:, None] < doc_ends[None, :])
    ).astype(jnp.bfloat16)
    all_weights = jnp.dot(member, routing, preferred_element_type=jnp.float32).astype(jnp.bfloat16)
    totals = lax.psum_scatter(
        outer_sum(all_weights, out_low, in_low), "tok", scatter_dimension=0, tiled=True
    )
    slot_lengths = jnp.sum(jnp.where(matches, doc_lengths[:, None], 0), axis=0)
    own_lengths = lax.dynamic_slice_in_dim(slot_lengths, own_first, slot_count, 0)
    scaling = lax.rsqrt(own_lengths.astype(jnp.float32))
    return totals * scaling[:, None, None]


def solution(mesh):
    in_specs = (
        P(("grp", "tok"), "feat"),
        P(("grp", "tok"), "feat"),
        P("feat", None),
        P("feat", None),
        P("grp"),
        P("grp"),
    )
    out_specs = P(("grp", "tok"), "feat", None)
    return jax.shard_map(shards, mesh=mesh, in_specs=in_specs, out_specs=out_specs, check_vma=False)
```

profile of v0, /device:TPU:0, one launch (start us, length us, event | category | flops | bytes accessed | tf_op | source)
XLA Modules:
  0.0 109.7 jit_solution(2129140301364226923)
XLA Ops:
  6.5 0.0 copy-start
  6.5 0.0 copy-start.1
  6.5 0.0 reduce-scatter.3.cloned.1.call-start
  6.5 1.9 %copy-done = bf16[768,2048]{1,0:T(8,128)(2,1)S(1)} copy-done((bf16[768,2048]{1,0:T(8,128)(2,1)S(1)}, bf16[768,2048]{1,0:T(8,128)(2,1)}, u32[]{:S(2)}) %copy-start) | copy-done | bytes 3145752
  8.4 4.5 %fusion.15 = f32[768,512]{1,0:T(8,128)} fusion(bf16[768,2048]{1,0:T(8,128)(2,1)S(1)} %copy-done, bf16[2048,512]{1,0:T(8,128)(2,1)} %param.9), kind=kOutput, calls=%fused_computation.23 | convolution fusion | flops 1610612736 | bytes 6815744 | tf_op jit(solution)/shard_map/dot_general | solution.py:24
  13.0 0.0 reduce-scatter.3.cloned.1.call-update
  13.0 0.0 reduce-scatter.5.cloned.1.call-start
  13.0 0.0 copy-done.1
  13.1 0.1 convert_reduce_fusion
  13.1 0.0 copy-start.2
  13.1 11.6 %fusion.16 = f32[768,512]{1,0:T(8,128)} fusion(bf16[768,7168]{1,0:T(8,128)(2,1)} %param.6, bf16[7168,512]{1,0:T(8,128)(2,1)} %param.8), kind=kOutput, calls=%fused_computation.24 | convolution fusion | flops 5637144576 | bytes 19922944 | tf_op jit(solution)/shard_map/dot_general | solution.py:23
  24.8 0.0 copy-done.2
  24.8 0.2 reduce-window.8
  25.0 0.3 convolution_convert_fusion
  25.2 43.7 %all-reduce.1 = bf16[768,512]{1,0:T(8,128)(2,1)} all-reduce(f32[768,512]{1,0:T(8,128)} %fusion.16), channel_id=1, replica_groups=mesh['grp'=2,'tok'=4,'feat'=4] {'feat'}, use_global_device_ids=true, to_apply=%region_3.4 | all-reduce | flops 393216 | bytes 2359296 | tf_op jit(solution)/shard_map/psum | solution.py:25
  68.9 0.0 reduce-scatter.3.cloned.1.call-done
  68.9 1.0 convert_element_type.17
  70.0 0.1 copy.9
  70.1 2.7 %fusion = f32[4,128,512]{2,1,0:T(8,128)} fusion(bf16[768,512]{1,0:T(8,128)(2,1)} %all-reduce.1, bf16[768,4]{0,1:T(4,128)(2,1)S(1)} %convolution_convert_fusion, bf16[768,128]{0,1:T(8,128)(2,1)S(1)} %copy.9), kind=kOutput, calls=%fused_computation.1 | convolution fusion | flops 403046400 | bytes 2037760 | tf_op jit(solution)/shard_map/dot_general | solution.py:13
  72.8 0.0 reduce-scatter.5.cloned.1.call-update
  72.8 0.1 select_reduce_fusion
  72.9 0.6 dynamic_slice.3
  74.2 26.9 %reduce-scatter.5.cloned.1.call-done = f32[1,128,512]{2,1,0:T(8,128)} async-done(((f32[4,128,512]{2,1,0:T(8,128)}), f32[1,128,512]{2,1,0:T(8,128)}) %reduce-scatter.5.cloned.1.call-update) | async-done | bytes 262160 | tf_op jit(solution)/shard_map/reduce_scatter | solution.py:44
  101.1 1.7 %broadcast_multiply_fusion = f32[1,128,512]{2,1,0:T(8,128)} fusion(f32[1,128,512]{2,1,0:T(8,128)} %reduce-scatter.5.cloned.1.call-done, f32[]{:T(128)} %bitcast.6), kind=kLoop, calls=%fused_computation.8 | loop fusion | flops 65536 | bytes 524292 | tf_op jit(solution)/shard_map/mul | solution.py:50
  (3 shorter events, 0.0 us)
Async XLA Ops:
  6.5 1.9 %copy-start = (bf16[768,2048]{1,0:T(8,128)(2,1)S(1)}, bf16[768,2048]{1,0:T(8,128)(2,1)}, u32[]{:S(2)}) copy-start(bf16[768,2048]{1,0:T(8,128)(2,1)} %param.7) | copy-start | bytes 9437188
  6.5 6.5 %copy-start.1 = (s32[4]{0:T(128)S(1)}, s32[4]{0:T(128)}, u32[]{:S(2)}) copy-start(s32[4]{0:T(128)} %param.11) | copy-start | bytes 52
  6.5 62.4 %reduce-scatter.3.cloned.1.call-start = ((), (), s32[]{:S(2)}) async-start(), calls=%async_computation.2 | async-start | bytes 1966080 | tf_op jit(solution)/shard_map/reduce_scatter | solution.py:26
  13.0 88.2 %reduce-scatter.5.cloned.1.call-start = ((), (), s32[]{:S(2)}) async-start(), calls=%async_computation.3 | async-start | bytes 1310720 | tf_op jit(solution)/shard_map/reduce_scatter | solution.py:44
  13.1 11.6 %copy-start.2 = (s32[4]{0:T(128)S(1)}, s32[4]{0:T(128)}, u32[]{:S(2)}) copy-start(s32[4]{0:T(128)} %param.10) | copy-start | bytes 52
Sparse Core Ops, SparseCore 0:
  13.1 39.2 reduce-scatter.2
  73.0 28.1 reduce-scatter.4
where the time goes:
time: 110 us
  blocking collectives  43.7 us (40%)
  waiting for transfers between devices  27 us (25%)
  matrix products  19.1 us (17%)
  between operations  14.1 us (13%)
  other arithmetic  3.05 us (3%)
  local copies, waits for them, and re-layouts  2.62 us (2%)
    psum x1, blocking collectives, shards(): full_in = lax.psum(part_in, 'feat')  43.7 us
    reduce_scatter x1, waiting for transfers between devices, shards(): lax.psum_scatter(outer_sum(all_weights, out_low, in_low), 'tok', scatter_...  26.9 us
    dot_general x1, matrix products, shards(): part_in = jnp.dot(acts, proj_in, preferred_element_type=jnp.float32)  11.6 us
    dot_general x1, matrix products, shards(): part_out = jnp.dot(grads, proj_out, preferred_element_type=jnp.float32)  4.54 us
    dot_general x1, matrix products, outer_sum(): lax.dot_general(weighted, low_in, (((0,), (0,)), ((), ())), preferred_ele...  2.7 us
  transfers between devices with their start and end apart: 2, of which 1 were waited for; matrix products, arithmetic and copies ran while one was open for 12% of the time, Pallas kernels for 0%

commit v1 on v0

--- a/solution.py
+++ b/solution.py
@@ -22,7 +22,12 @@
     slot_count = doc_count // lax.axis_size("tok")
     part_in = jnp.dot(acts, proj_in, preferred_element_type=jnp.float32)
     part_out = jnp.dot(grads, proj_out, preferred_element_type=jnp.float32)
-    full_in = lax.psum(part_in, "feat")
+    n = jax.lax.psum(1, "feat")
+    full_in, inter = (part_in, 0)
+    while 1 << inter < n:
+        finding = jax.lax.ppermute(full_in, "feat", [(k0, k0 ^ 1 << inter) for k0 in range(n)])
+        full_in = full_in + finding
+        inter = inter + 1
     grad_part = lax.psum_scatter(part_out, "feat", scatter_dimension=1, tiled=True)
     in_low = full_in.astype(jnp.bfloat16)
     out_low = grad_part.astype(jnp.bfloat16)

time: 110 us -> 116 us (1.055)
  waiting for transfers between devices: 27 us -> 72.2 us
  blocking collectives: 43.7 us -> 0 us
  starting transfers between devices: 0.04 us -> 3.44 us
  other arithmetic: 3.05 us -> 4.55 us
    psum x1 -> x0, blocking collectives: 43.7 us -> none  [shards(): full_in = lax.psum(part_in, 'feat')]
    ppermute x0 -> x2, waiting for transfers between devices: none -> 24.6 us  [shards(): jax.lax.ppermute(full_in, 'feat', [(k0, k0 ^ 1 << inter) for k0 in range(...]
    reduce_scatter x1, waiting for transfers between devices: 0.01 us -> 20.1 us  [shards(): lax.psum_scatter(part_out, 'feat', scatter_dimension=1, tiled=True)]
    ppermute x0 -> x2, starting transfers between devices: none -> 3.39 us  [shards(): jax.lax.ppermute(full_in, 'feat', [(k0, k0 ^ 1 << inter) for k0 in range(...]
    add x0 -> x1, other arithmetic: none -> 1.49 us  [shards(): full_in = full_in + finding]
  transfers between devices with their start and end apart: 2 -> 4, of which waited for: 1 -> 4; matrix products, arithmetic and copies ran while one was open for 12% -> 13% of each run, Pallas kernels for 0% -> 0%
where the time goes in v1:
time: 116 us
  waiting for transfers between devices  72.2 us (62%)
  matrix products  19 us (16%)
  between operations  14.1 us (12%)
  other arithmetic  4.55 us (4%)
  starting transfers between devices  3.44 us (3%)
  local copies, waits for them, and re-layouts  2.63 us (2%)
    reduce_scatter x1, waiting for transfers between devices, shards(): lax.psum_scatter(outer_sum(all_weights, out_low, in_low), 'tok', scatter_...  27.4 us
    ppermute x2, waiting for transfers between devices, shards(): jax.lax.ppermute(full_in, 'feat', [(k0, k0 ^ 1 << inter) for k0 in range(...  24.6 us
    reduce_scatter x1, waiting for transfers between devices, shards(): lax.psum_scatter(part_out, 'feat', scatter_dimension=1, tiled=True)  20.1 us
    dot_general x1, matrix products, shards(): part_in = jnp.dot(acts, proj_in, preferred_element_type=jnp.float32)  10.7 us
    dot_general x1, matrix products, shards(): part_out = jnp.dot(grads, proj_out, preferred_element_type=jnp.float32)  4.52 us
    dot_general x1, matrix products, outer_sum(): lax.dot_general(weighted, low_in, (((0,), (0,)), ((), ())), preferred_ele...  3.46 us
    ppermute x2, starting transfers between devices, shards(): jax.lax.ppermute(full_in, 'feat', [(k0, k0 ^ 1 << inter) for k0 in range(...  3.39 us
  transfers between devices with their start and end apart: 4, of which 4 were waited for; matrix products, arithmetic and copies ran while one was open for 13% of the time, Pallas kernels for 0%

profile of v1, /device:TPU:0, one launch (start us, length us, event | category | flops | bytes accessed | tf_op | source)
XLA Modules:
  0.0 116.0 jit_solution(6427225293190634455)
XLA Ops:
  6.5 0.0 copy-start
  6.5 0.0 reduce-scatter.3.cloned.1.call-start
  6.5 1.9 %copy-done = bf16[768,2048]{1,0:T(8,128)(2,1)S(1)} copy-done((bf16[768,2048]{1,0:T(8,128)(2,1)S(1)}, bf16[768,2048]{1,0:T(8,128)(2,1)}, u32[]{:S(2)}) %copy-start) | copy-done | bytes 3145752
  8.4 4.5 %fusion.15 = f32[768,512]{1,0:T(8,128)} fusion(bf16[768,2048]{1,0:T(8,128)(2,1)S(1)} %copy-done, bf16[2048,512]{1,0:T(8,128)(2,1)} %param.9), kind=kOutput, calls=%fused_computation.23 | convolution fusion | flops 1610612736 | bytes 6815744 | tf_op jit(solution)/shard_map/dot_general | solution.py:24
  12.9 0.0 reduce-scatter.3.cloned.1.call-update
  13.0 0.0 reduce-scatter.5.cloned.1.call-start
  13.0 10.7 %fusion.16 = f32[768,512]{1,0:T(8,128)S(1)} fusion(bf16[768,7168]{1,0:T(8,128)(2,1)} %param.6, bf16[7168,512]{1,0:T(8,128)(2,1)} %param.8), kind=kOutput, calls=%fused_computation.24 | convolution fusion | flops 5637144576 | bytes 19922944 | tf_op jit(solution)/shard_map/dot_general | solution.py:23
  23.8 0.0 copy-start.1
  23.8 0.0 copy-start.2
  23.8 0.6 collective-permute-start
  24.3 3.0 %collective-permute-done = f32[768,512]{1,0:T(8,128)S(1)} collective-permute-done((f32[768,512]{1,0:T(8,128)S(1)}, f32[768,512]{1,0:T(8,128)S(1)}, u32[]{:S(2)}, u32[]{:S(2)}) %collective-permute-start) | collective-permute-done | bytes 1572896 | tf_op jit(solution)/shard_map/ppermute | solution.py:28
  27.4 1.5 %add.29 = f32[768,512]{1,0:T(8,128)} add(f32[768,512]{1,0:T(8,128)S(1)} %fusion.16, f32[768,512]{1,0:T(8,128)S(1)} %collective-permute-done) | non-fusion elementwise | flops 393216 | bytes 4718592 | tf_op jit(solution)/shard_map/add | solution.py:29
  28.9 2.8 %collective-permute-start.1 = (f32[768,512]{1,0:T(8,128)}, f32[768,512]{1,0:T(8,128)}, u32[]{:S(2)}, u32[]{:S(2)}) collective-permute-start(f32[768,512]{1,0:T(8,128)} %add.29), channel_id=1, source_target_pairs={{0,2},{1,3},{2,0},{3,1},{4,6},{5,7},{6,4},{7,5},{8,10},{9,11},{10,... | collective-permute-start | bytes 4718600 | tf_op jit(solution)/shard_map/ppermute | solution.py:28
  31.7 0.0 copy-done.1
  31.7 0.1 convert_reduce_fusion
  31.8 0.0 copy-done.2
  31.8 0.2 reduce-window.8
  32.0 0.3 convolution_convert_fusion
  32.3 20.1 %reduce-scatter.3.cloned.1.call-done = f32[768,128]{1,0:T(8,128)} async-done(((f32[768,512]{1,0:T(8,128)}), f32[768,128]{1,0:T(8,128)}) %reduce-scatter.3.cloned.1.call-update) | async-done | bytes 393232 | tf_op jit(solution)/shard_map/reduce_scatter | solution.py:31
  52.4 1.0 convert_element_type.17
  53.4 0.1 copy.9
  53.6 21.6 %collective-permute-done.1 = f32[768,512]{1,0:T(8,128)} collective-permute-done((f32[768,512]{1,0:T(8,128)}, f32[768,512]{1,0:T(8,128)}, u32[]{:S(2)}, u32[]{:S(2)}) %collective-permute-start.1) | collective-permute-done | bytes 1572896 | tf_op jit(solution)/shard_map/ppermute | solution.py:28
  75.2 3.5 %fusion.1 = f32[4,128,512]{2,1,0:T(8,128)} fusion(f32[768,512]{1,0:T(8,128)} %add.29, f32[768,512]{1,0:T(8,128)} %collective-permute-done.1, bf16[768,4]{0,1:T(4,128)(2,1)S(1)} %convolution_convert_fusion, bf16[768,128]{0,1:T(8,128)(2,1)S(1)} %copy.9), kind=kOutput, calls=%fused_computation.3 | convolution fusion | flops 403832832 | bytes 4397056 | tf_op jit(solution)/shard_map/dot_general | solution.py:13
  78.6 0.0 reduce-scatter.5.cloned.1.call-update
  78.6 0.1 select_reduce_fusion
  78.7 0.6 dynamic_slice.3
  80.0 27.4 %reduce-scatter.5.cloned.1.call-done = f32[1,128,512]{2,1,0:T(8,128)} async-done(((f32[4,128,512]{2,1,0:T(8,128)}), f32[1,128,512]{2,1,0:T(8,128)}) %reduce-scatter.5.cloned.1.call-update) | async-done | bytes 262160 | tf_op jit(solution)/shard_map/reduce_scatter | solution.py:49
  107.5 1.7 %broadcast_multiply_fusion = f32[1,128,512]{2,1,0:T(8,128)} fusion(f32[1,128,512]{2,1,0:T(8,128)} %reduce-scatter.5.cloned.1.call-done, f32[]{:T(128)} %bitcast.6), kind=kLoop, calls=%fused_computation.8 | loop fusion | flops 65536 | bytes 524292 | tf_op jit(solution)/shard_map/mul | solution.py:55
  (3 shorter events, 0.0 us)
Async XLA Ops:
  6.5 1.9 %copy-start = (bf16[768,2048]{1,0:T(8,128)(2,1)S(1)}, bf16[768,2048]{1,0:T(8,128)(2,1)}, u32[]{:S(2)}) copy-start(bf16[768,2048]{1,0:T(8,128)(2,1)} %param.7) | copy-start | bytes 9437188
  6.5 45.9 %reduce-scatter.3.cloned.1.call-start = ((), (), s32[]{:S(2)}) async-start(), calls=%async_computation.2 | async-start | bytes 1966080 | tf_op jit(solution)/shard_map/reduce_scatter | solution.py:31
  13.0 94.5 %reduce-scatter.5.cloned.1.call-start = ((), (), s32[]{:S(2)}) async-start(), calls=%async_computation.3 | async-start | bytes 1310720 | tf_op jit(solution)/shard_map/reduce_scatter | solution.py:49
  23.8 8.0 %copy-start.1 = (s32[4]{0:T(128)S(1)}, s32[4]{0:T(128)}, u32[]{:S(2)}) copy-start(s32[4]{0:T(128)} %param.11) | copy-start | bytes 52
  23.8 8.0 %copy-start.2 = (s32[4]{0:T(128)S(1)}, s32[4]{0:T(128)}, u32[]{:S(2)}) copy-start(s32[4]{0:T(128)} %param.10) | copy-start | bytes 52
  23.8 3.6 %collective-permute-start = (f32[768,512]{1,0:T(8,128)S(1)}, f32[768,512]{1,0:T(8,128)S(1)}, u32[]{:S(2)}, u32[]{:S(2)}) collective-permute-start(f32[768,512]{1,0:T(8,128)S(1)} %fusion.16), channel_id=1, source_target_pairs={{0,1},{1,0},{2,3},{3,2},{4,5},{5,4},{6,7},{7,6},{8,9},{9,8},{10,11... | collective-permute-start | bytes 4718600 | tf_op jit(solution)/shard_map/ppermute | solution.py:28
  28.9 46.3 %collective-permute-start.1 = (f32[768,512]{1,0:T(8,128)}, f32[768,512]{1,0:T(8,128)}, u32[]{:S(2)}, u32[]{:S(2)}) collective-permute-start(f32[768,512]{1,0:T(8,128)} %add.29), channel_id=1, source_target_pairs={{0,2},{1,3},{2,0},{3,1},{4,6},{5,7},{6,4},{7,5},{8,10},{9,11},{10,... | collective-permute-start | bytes 4718600 | tf_op jit(solution)/shard_map/ppermute | solution.py:28
Sparse Core Ops, SparseCore 0:
  13.1 39.2 reduce-scatter.2
  78.8 28.6 reduce-scatter.4
